TPU v7x, 256 devices: a whole 4x4x8 slice. The times are simulated.
256 devices in a mesh: row: 8 (over y, core), col: 32 (over x, z).
Axes of the slice: x: 4, y: 4, z: 8, core: 2. Of those that a mesh axis runs over, the one named last changes fastest.
Arguments:
- x_blocks: bfloat16 [8, 32, 42, 128, 128], P('row', 'col'), may hold values from -1.1953125 to 1.1953125
- x_slots: int32 [8, 32, 42], replicated, may hold values from 0 to 255, as said below
- x_count: int32 [8, 32], replicated, may hold values from 21 to 42, as said below
- s_slots: int32 [8, 32, 2], replicated, may hold values from 0 to 15, as said below
- s_count: int32 [8, 32], replicated, may hold values from 1 to 2, as said below
Outputs:
- square_blocks: bfloat16 [8, 32, 2, 128, 128], P('row', 'col')
- result_blocks: bfloat16 [8, 32, 2, 128, 128], P('row', 'col')
Inputs may be any that keep to these rules, and one draw needn't show every extreme that they name: `x_slots`: in each tile the live slots hold distinct positions; the live blocks whose position % 32 is below 2 come first among the live slots, at most 2 of them, and some tile has exactly 2. Positions of slots that are not live are arbitrary within the range. `x_count`: some tile has exactly 42 live slots. `s_slots`: in each tile the live slots hold distinct positions. `s_count`: some tile has exactly 2 live slots.
All inputs are finite; a program needn't handle non-finite values.
Results may differ from a plain program's by a relative error of at most 0.0049.
Values may be sent and summed in bfloat16 or wider, within the bound.
A program may use at most 128 MiB of HBM per device.

v0:
```python
import math

import jax
import jax.numpy as jnp
from jax import lax
from jax.sharding import PartitionSpec as P

RB = 8
JW = 2
CAPW = 2


def laid_out(pieces, dim):
    dims = list(pieces.shape[1:])
    dims[dim] *= pieces.shape[0]
    return jnp.moveaxis(pieces, 0, dim).reshape(dims)


def copy_for_each(array, axis):
    length = lax.axis_size(axis)
    return lax.all_to_all(
        jnp.broadcast_to(array[None], (length, *array.shape)), axis, 0, 0, tiled=True
    )


def gathered_copies(array, axis, dim):
    return laid_out(copy_for_each(array, axis), dim)


def match_index(targets, slot_keys, slot_live):
    matches = (targets[..., None] == slot_keys) & slot_live
    ordinal = jnp.arange(1, slot_keys.shape[0] + 1, dtype=jnp.int32)
    located = jnp.sum(jnp.where(matches, ordinal, 0), axis=-1)
    return jnp.where(located > 0, located - 1, slot_keys.shape[0])


def local(x_blocks, x_slots, x_count, s_slots, s_count):
    row_total = lax.axis_size("row")
    col_total = lax.axis_size("col")
    row_id = lax.axis_index("row")
    col_id = lax.axis_index("col")
    capacity = x_blocks.shape[2]
    block_size = x_blocks.shape[3]
    order_blocks = RB * col_total
    tile_width = order_blocks // row_total
    panel_all = lax.all_gather(x_blocks, "row", axis=0, tiled=True)
    stacked = panel_all.reshape(row_total * capacity, block_size, block_size)
    padded = jnp.concatenate(
        [stacked, jnp.zeros((1, block_size, block_size), stacked.dtype)], axis=0
    )
    column_slots = lax.dynamic_index_in_dim(x_slots, col_id, 1, keepdims=False)
    column_count = lax.dynamic_index_in_dim(x_count, col_id, 1, keepdims=False)
    ordinal = jnp.arange(capacity, dtype=jnp.int32)
    panel_live = (ordinal[None, :] < column_count[:, None]).reshape(-1)
    owners = jnp.arange(row_total, dtype=jnp.int32)[:, None]
    panel_keys = (
        column_slots // tile_width * order_blocks + owners * tile_width + column_slots % tile_width
    ).reshape(-1)
    row_lanes = jnp.arange(RB, dtype=jnp.int32)
    window_ids = jnp.arange(JW, dtype=jnp.int32)

    def accumulate(running, values, inner_row, inner_col, usable):
        picked = match_index(
            row_lanes[None, :] * order_blocks + inner_row[:, None], panel_keys, panel_live
        )
        left_part = jnp.take(padded, picked, axis=0)
        placing = ((inner_col[:, None] == window_ids[None, :]) & usable[:, None]).astype(
            values.dtype
        )
        placed = placing[:, :, None, None] * values[:, None, :, :]
        return running + jnp.einsum(
            "nrxy,njyz->rjxz", left_part, placed, preferred_element_type=jnp.float32
        )

    def make_step(slot_table, count_row, stride, column_limit):

        def fold_step(running, piece, offset):
            pieces = piece.shape[1]
            slot_count = piece.shape[2]
            positions = lax.dynamic_slice_in_dim(slot_table, offset, pieces, 0)[:, :slot_count]
            counts = lax.dynamic_slice_in_dim(count_row, offset, pieces, 0)
            owner_ids = offset + jnp.arange(pieces, dtype=jnp.int32)[:, None]
            inner_row = owner_ids * RB + positions // stride
            inner_col = positions % stride
            usable = (jnp.arange(slot_count, dtype=jnp.int32)[None, :] < counts[:, None]) & (
                inner_col < column_limit
            )
            values = piece.reshape(pieces * slot_count, block_size, block_size)
            return accumulate(
                running, values, inner_row.reshape(-1), inner_col.reshape(-1), usable.reshape(-1)
            )

        return fold_step

    blank_sum = jnp.zeros((RB, JW, block_size, block_size), jnp.float32)

    def collect_all(gathered, fold_step):
        per_turn = math.gcd(col_total, 8)

        def advance(turn_index, running):
            offset = turn_index * per_turn
            portion = lax.dynamic_slice_in_dim(gathered, offset, per_turn, 1)
            return fold_step(running, portion, offset)

        return lax.fori_loop(0, col_total // per_turn, advance, blank_sum)

    row_slots = lax.dynamic_index_in_dim(x_slots, row_id, 0, keepdims=False)
    row_count = lax.dynamic_index_in_dim(x_count, row_id, 0, keepdims=False)
    square_slots = lax.dynamic_index_in_dim(s_slots, row_id, 0, keepdims=False)
    square_count = lax.dynamic_index_in_dim(s_count, row_id, 0, keepdims=False)
    window_part = x_blocks[:, :, :CAPW]
    first_step = make_step(row_slots, row_count, tile_width, JW)
    product = collect_all(gathered_copies(window_part, "col", 1), first_step)
    own_slots = lax.dynamic_index_in_dim(square_slots, col_id, 0, keepdims=False)
    own_count = lax.dynamic_index_in_dim(square_count, col_id, 0, keepdims=False)
    own_live = jnp.arange(own_slots.shape[0], dtype=jnp.int32) < own_count
    flat_one = product.reshape(RB * JW, block_size, block_size)
    square_part = jnp.where(
        own_live[:, None, None], jnp.take(flat_one, own_slots, axis=0), 0.0
    ).astype(jnp.bfloat16)
    square_part = square_part[None, None]
    second_step = make_step(square_slots, square_count, JW, JW)
    second = collect_all(gathered_copies(square_part, "col", 1), second_step)
    own_keys = own_slots // JW * order_blocks + row_id * tile_width + own_slots % JW
    own_block = jnp.take(padded, match_index(own_keys, panel_keys, panel_live), axis=0).astype(
        jnp.float32
    )
    flat_two = second.reshape(RB * JW, block_size, block_size)
    combined = 1.5 * own_block - 0.5 * jnp.take(flat_two, own_slots, axis=0)
    result = jnp.where(own_live[:, None, None], combined, 0.0).astype(jnp.bfloat16)
    return (square_part, result[None, None])


def solution(mesh):
    in_specs = (P("row", "col", None, None, None), P(), P(), P(), P())
    out_specs = (P("row", "col", None, None, None), P("row", "col", None, None, None))
    return jax.shard_map(local, mesh=mesh, in_specs=in_specs, out_specs=out_specs, check_vma=False)
```

profile of v0, /device:TPU:1, one launch (start us, length us, event | category | flops | bytes accessed | tf_op | source)
XLA Modules:
  0.0 268.8 jit_solution(12169378988364675214)
XLA Ops:
  10.8 11.9 %all-to-all-start = ((bf16[32,1,1,2,128,128]{4,5,3,2,1,0:T(8,128)(2,1)}), bf16[32,1,1,2,128,128]{4,5,3,2,1,0:T(8,128)(2,1)S(1)}, u32[]{:S(2)}, u32[]{:S(2)}) async-start(bf16[32,1,1,2,128,128]{4,5,3,2,1,0:T(8,128)(2,1)} %broadcast_in_dim.199), calls=%async_computation | async-start | bytes 4194304 | tf_op jit(solution)/shard_map/all_to_all | solution.py:21
  28.4 48.9 %all-gather.2.cloned.1.call-done = bf16[8,1,42,128,128]{4,3,2,1,0:T(8,128)(2,1)} async-done(((bf16[1,1,42,128,128]{4,3,2,1,0:T(8,128)(2,1)}), bf16[8,1,42,128,128]{4,3,2,1,0:T(8,128)(2,1)}) %all-gather.2.cloned.1.call-update) | async-done | bytes 11010064 | tf_op jit(solution)/shard_map/all_gather | solution.py:46
  77.3 10.6 %concatenate.3 = bf16[337,128,128]{2,1,0:T(8,128)(2,1)} pad(bf16[336,128,128]{2,1,0:T(8,128)(2,1)} %bitcast.101, bf16[]{:T(256)} %constant.410.clone.1), padding=0_1x0_0x0_0 | pad | bytes 22052866 | tf_op jit(solution)/shard_map/concatenate | solution.py:48
  87.9 54.0 %while.36 = (s32[]{:T(128)}, f32[8,2,128,128]{2,3,0,1:T(8,128)}, s32[32,42]{1,0:T(8,128)S(1)}, s32[32]{0:T(128)S(1)}, bf16[1,32,2,128,128]{3,4,2,1,0:T(8,128)(2,...) while((s32[]{:T(128)}, f32[8,2,128,128]{2,3,0,1:T(8,128)}, ...), condition=%wide.wide.region_2.4_spmd.clone, body=%wide.wide.region_0.3_spmd.clone.sunk | while | flops 1078636672 | bytes 16272037 | solution.py:105
  89.0 7.3 %gather_fusion = bf16[128,128,128]{2,1,0:T(8,128)(2,1)} fusion(bf16[337,128,128]{2,1,0:T(8,128)(2,1)} %get-tuple-element.924, s32[1024]{0:T(1024)S(1)} %pad_clamp_fusion.8), kind=kCustom, calls=%fused_computation.clone.clone.clone.1 | custom fusion | bytes 8389120 | tf_op jit(solution)/shard_map/while/body/eval_jaxpr/jit(_take)/gather | solution.py:66
  96.6 4.6 %fusion.100 = f32[8,2,128,128]{2,3,0,1:T(8,128)} fusion(bf16[16,8,128,128]{3,2,1,0:T(8,128)(2,1)} %bitcast.97, pred[16,8]{0,1:T(8,128)(4,1)S(1)} %copy.73, f32[8,2,128,128]{2,3,0,1:T(8,128)} %get-tuple-element.906, bf16[16,128,128]{1,2,0:T(8,128)(2,1)S(1)} %bitcast.99, bf16[16,2]{0,1:T(2,128)(2,1)S(1)} %and_convert_fusion.6, pred[]{:T(512)S(6)} %compare.58), kind=kOutput, calls=%fused_computation.17.clone.clone.1 | convolution fusion | flops 1078460416 | bytes 6815937 | tf_op jit(solution)/shard_map/while/body/eval_jaxpr/nrxy,njyz->rjxz/dot_general | solution.py:71
  102.3 7.3 %gather_fusion = bf16[128,128,128]{2,1,0:T(8,128)(2,1)} fusion(bf16[337,128,128]{2,1,0:T(8,128)(2,1)} %get-tuple-element.924, s32[1024]{0:T(1024)S(1)} %pad_clamp_fusion.8), kind=kCustom, calls=%fused_computation.clone.clone.clone.1 | custom fusion | bytes 8389120 | tf_op jit(solution)/shard_map/while/body/eval_jaxpr/jit(_take)/gather | solution.py:66
  109.9 4.8 %fusion.100 = f32[8,2,128,128]{2,3,0,1:T(8,128)} fusion(bf16[16,8,128,128]{3,2,1,0:T(8,128)(2,1)} %bitcast.97, pred[16,8]{0,1:T(8,128)(4,1)S(1)} %copy.73, f32[8,2,128,128]{2,3,0,1:T(8,128)} %get-tuple-element.906, bf16[16,128,128]{1,2,0:T(8,128)(2,1)S(1)} %bitcast.99, bf16[16,2]{0,1:T(2,128)(2,1)S(1)} %and_convert_fusion.6, pred[]{:T(512)S(6)} %compare.58), kind=kOutput, calls=%fused_computation.17.clone.clone.1 | convolution fusion | flops 1078460416 | bytes 6815937 | tf_op jit(solution)/shard_map/while/body/eval_jaxpr/nrxy,njyz->rjxz/dot_general | solution.py:71
  115.9 7.3 %gather_fusion = bf16[128,128,128]{2,1,0:T(8,128)(2,1)} fusion(bf16[337,128,128]{2,1,0:T(8,128)(2,1)} %get-tuple-element.924, s32[1024]{0:T(1024)S(1)} %pad_clamp_fusion.8), kind=kCustom, calls=%fused_computation.clone.clone.clone.1 | custom fusion | bytes 8389120 | tf_op jit(solution)/shard_map/while/body/eval_jaxpr/jit(_take)/gather | solution.py:66
  123.5 4.8 %fusion.100 = f32[8,2,128,128]{2,3,0,1:T(8,128)} fusion(bf16[16,8,128,128]{3,2,1,0:T(8,128)(2,1)} %bitcast.97, pred[16,8]{0,1:T(8,128)(4,1)S(1)} %copy.73, f32[8,2,128,128]{2,3,0,1:T(8,128)} %get-tuple-element.906, bf16[16,128,128]{1,2,0:T(8,128)(2,1)S(1)} %bitcast.99, bf16[16,2]{0,1:T(2,128)(2,1)S(1)} %and_convert_fusion.6, pred[]{:T(512)S(6)} %compare.58), kind=kOutput, calls=%fused_computation.17.clone.clone.1 | convolution fusion | flops 1078460416 | bytes 6815937 | tf_op jit(solution)/shard_map/while/body/eval_jaxpr/nrxy,njyz->rjxz/dot_general | solution.py:71
  129.4 7.3 %gather_fusion = bf16[128,128,128]{2,1,0:T(8,128)(2,1)} fusion(bf16[337,128,128]{2,1,0:T(8,128)(2,1)} %get-tuple-element.924, s32[1024]{0:T(1024)S(1)} %pad_clamp_fusion.8), kind=kCustom, calls=%fused_computation.clone.clone.clone.1 | custom fusion | bytes 8389120 | tf_op jit(solution)/shard_map/while/body/eval_jaxpr/jit(_take)/gather | solution.py:66
  137.0 4.8 %fusion.100 = f32[8,2,128,128]{2,3,0,1:T(8,128)} fusion(bf16[16,8,128,128]{3,2,1,0:T(8,128)(2,1)} %bitcast.97, pred[16,8]{0,1:T(8,128)(4,1)S(1)} %copy.73, f32[8,2,128,128]{2,3,0,1:T(8,128)} %get-tuple-element.906, bf16[16,128,128]{1,2,0:T(8,128)(2,1)S(1)} %bitcast.99, bf16[16,2]{0,1:T(2,128)(2,1)S(1)} %and_convert_fusion.6, pred[]{:T(512)S(6)} %compare.58), kind=kOutput, calls=%fused_computation.17.clone.clone.1 | convolution fusion | flops 1078460416 | bytes 6815937 | tf_op jit(solution)/shard_map/while/body/eval_jaxpr/nrxy,njyz->rjxz/dot_general | solution.py:71
  146.0 9.6 %all-to-all-start.1 = ((bf16[32,1,1,2,128,128]{4,5,3,2,1,0:T(8,128)(2,1)}), bf16[32,1,1,2,128,128]{4,5,3,2,1,0:T(8,128)(2,1)S(1)}, u32[]{:S(2)}, u32[]{:S(2)}) async-start(bf16[32,1,1,2,128,128]{4,5,3,2,1,0:T(8,128)(2,1)} %broadcast_in_dim.207), calls=%async_computation.1 | async-start | bytes 4194304 | tf_op jit(solution)/shard_map/all_to_all | solution.py:21
  156.4 4.7 %gather_fusion.2 = bf16[2,128,128]{2,1,0:T(8,128)(2,1)S(1)} fusion(bf16[337,128,128]{2,1,0:T(8,128)(2,1)} %get-tuple-element.971, s32[1024]{0:T(1024)S(1)} %pad_clamp_fusion.2), kind=kCustom, calls=%fused_computation.4 | custom fusion | bytes 131080 | tf_op jit(solution)/shard_map/jit(_take)/gather | solution.py:125
  161.8 42.7 %all-to-all-done.1 = bf16[32,1,1,2,128,128]{4,5,3,2,1,0:T(8,128)(2,1)S(1)} async-done(((bf16[32,1,1,2,128,128]{4,5,3,2,1,0:T(8,128)(2,1)}), bf16[32,1,1,2,128,128]{4,5,3,2,1,0:T(8,128)(2,1)S(1)}, u32[]{:S(2)}, u32[]{:S(2)}) %all-to-all-start.1) | async-done | bytes 2097184 | tf_op jit(solution)/shard_map/all_to_all | solution.py:21
  204.5 54.6 %while.37 = (s32[]{:T(128)}, f32[8,2,128,128]{2,3,0,1:T(8,128)}, s32[32,2]{0,1:T(2,128)S(1)}, s32[32]{0:T(128)S(1)}, bf16[1,32,2,128,128]{3,4,2,1,0:T(8,128)(2,1...) while((s32[]{:T(128)}, f32[8,2,128,128]{2,3,0,1:T(8,128)}, ...), condition=%wide.wide.region_6.9_spmd.clone, body=%wide.wide.region_4.8_spmd.clone.sunk | while | flops 1078636672 | bytes 16269573 | solution.py:105
  206.0 7.3 %gather_fusion.1 = bf16[128,128,128]{2,1,0:T(8,128)(2,1)} fusion(bf16[337,128,128]{2,1,0:T(8,128)(2,1)} %get-tuple-element.963, s32[1024]{0:T(1024)S(1)} %pad_clamp_fusion.9), kind=kCustom, calls=%fused_computation.2.clone.clone.clone.1 | custom fusion | bytes 8389120 | tf_op jit(solution)/shard_map/while/body/eval_jaxpr/jit(_take)/gather | solution.py:66
  213.4 4.6 %fusion.105 = f32[8,2,128,128]{2,3,0,1:T(8,128)} fusion(bf16[16,8,128,128]{3,2,1,0:T(8,128)(2,1)} %bitcast.98, pred[16,8]{0,1:T(8,128)(4,1)S(1)} %copy.76, f32[8,2,128,128]{2,3,0,1:T(8,128)} %get-tuple-element.945, bf16[16,128,128]{1,2,0:T(8,128)(2,1)S(1)} %bitcast.100, bf16[16,2]{0,1:T(2,128)(2,1)S(1)} %and_convert_fusion.7, pred[]{:T(512)S(6)} %compare.59), kind=kOutput, calls=%fused_computation.53.clone.clone.1 | convolution fusion | flops 1078460416 | bytes 6815937 | tf_op jit(solution)/shard_map/while/body/eval_jaxpr/nrxy,njyz->rjxz/dot_general | solution.py:71
  219.4 7.3 %gather_fusion.1 = bf16[128,128,128]{2,1,0:T(8,128)(2,1)} fusion(bf16[337,128,128]{2,1,0:T(8,128)(2,1)} %get-tuple-element.963, s32[1024]{0:T(1024)S(1)} %pad_clamp_fusion.9), kind=kCustom, calls=%fused_computation.2.clone.clone.clone.1 | custom fusion | bytes 8389120 | tf_op jit(solution)/shard_map/while/body/eval_jaxpr/jit(_take)/gather | solution.py:66
  226.8 4.8 %fusion.105 = f32[8,2,128,128]{2,3,0,1:T(8,128)} fusion(bf16[16,8,128,128]{3,2,1,0:T(8,128)(2,1)} %bitcast.98, pred[16,8]{0,1:T(8,128)(4,1)S(1)} %copy.76, f32[8,2,128,128]{2,3,0,1:T(8,128)} %get-tuple-element.945, bf16[16,128,128]{1,2,0:T(8,128)(2,1)S(1)} %bitcast.100, bf16[16,2]{0,1:T(2,128)(2,1)S(1)} %and_convert_fusion.7, pred[]{:T(512)S(6)} %compare.59), kind=kOutput, calls=%fused_computation.53.clone.clone.1 | convolution fusion | flops 1078460416 | bytes 6815937 | tf_op jit(solution)/shard_map/while/body/eval_jaxpr/nrxy,njyz->rjxz/dot_general | solution.py:71
  233.1 7.3 %gather_fusion.1 = bf16[128,128,128]{2,1,0:T(8,128)(2,1)} fusion(bf16[337,128,128]{2,1,0:T(8,128)(2,1)} %get-tuple-element.963, s32[1024]{0:T(1024)S(1)} %pad_clamp_fusion.9), kind=kCustom, calls=%fused_computation.2.clone.clone.clone.1 | custom fusion | bytes 8389120 | tf_op jit(solution)/shard_map/while/body/eval_jaxpr/jit(_take)/gather | solution.py:66
  240.5 4.8 %fusion.105 = f32[8,2,128,128]{2,3,0,1:T(8,128)} fusion(bf16[16,8,128,128]{3,2,1,0:T(8,128)(2,1)} %bitcast.98, pred[16,8]{0,1:T(8,128)(4,1)S(1)} %copy.76, f32[8,2,128,128]{2,3,0,1:T(8,128)} %get-tuple-element.945, bf16[16,128,128]{1,2,0:T(8,128)(2,1)S(1)} %bitcast.100, bf16[16,2]{0,1:T(2,128)(2,1)S(1)} %and_convert_fusion.7, pred[]{:T(512)S(6)} %compare.59), kind=kOutput, calls=%fused_computation.53.clone.clone.1 | convolution fusion | flops 1078460416 | bytes 6815937 | tf_op jit(solution)/shard_map/while/body/eval_jaxpr/nrxy,njyz->rjxz/dot_general | solution.py:71
  246.8 7.3 %gather_fusion.1 = bf16[128,128,128]{2,1,0:T(8,128)(2,1)} fusion(bf16[337,128,128]{2,1,0:T(8,128)(2,1)} %get-tuple-element.963, s32[1024]{0:T(1024)S(1)} %pad_clamp_fusion.9), kind=kCustom, calls=%fused_computation.2.clone.clone.clone.1 | custom fusion | bytes 8389120 | tf_op jit(solution)/shard_map/while/body/eval_jaxpr/jit(_take)/gather | solution.py:66
  254.2 4.8 %fusion.105 = f32[8,2,128,128]{2,3,0,1:T(8,128)} fusion(bf16[16,8,128,128]{3,2,1,0:T(8,128)(2,1)} %bitcast.98, pred[16,8]{0,1:T(8,128)(4,1)S(1)} %copy.76, f32[8,2,128,128]{2,3,0,1:T(8,128)} %get-tuple-element.945, bf16[16,128,128]{1,2,0:T(8,128)(2,1)S(1)} %bitcast.100, bf16[16,2]{0,1:T(2,128)(2,1)S(1)} %and_convert_fusion.7, pred[]{:T(512)S(6)} %compare.59), kind=kOutput, calls=%fused_computation.53.clone.clone.1 | convolution fusion | flops 1078460416 | bytes 6815937 | tf_op jit(solution)/shard_map/while/body/eval_jaxpr/nrxy,njyz->rjxz/dot_general | solution.py:71
  (224 shorter events, 29.5 us)
Async XLA Ops:
  7.2 18.2 %copy-start = (s32[8,32,2]{1,2,0:T(2,128)S(1)}, s32[8,32,2]{1,2,0:T(2,128)}, u32[]{:S(2)}) copy-start(s32[8,32,2]{1,2,0:T(2,128)} %param.16) | copy-start | bytes 6148
  7.2 17.6 %copy-start.3 = (s32[8,32]{1,0:T(8,128)S(1)}, s32[8,32]{1,0:T(8,128)}, u32[]{:S(2)}) copy-start(s32[8,32]{1,0:T(8,128)} %param.15) | copy-start | bytes 3076
  7.2 70.1 %all-gather.2.cloned.1.call-start = ((), (), s32[]{:S(2)}) async-start(), calls=%async_computation.2 | async-start | bytes 12386304 | tf_op jit(solution)/shard_map/all_gather | solution.py:46
  10.8 77.2 %all-to-all-start = ((bf16[32,1,1,2,128,128]{4,5,3,2,1,0:T(8,128)(2,1)}), bf16[32,1,1,2,128,128]{4,5,3,2,1,0:T(8,128)(2,1)S(1)}, u32[]{:S(2)}, u32[]{:S(2)}) async-start(bf16[32,1,1,2,128,128]{4,5,3,2,1,0:T(8,128)(2,1)} %broadcast_in_dim.199), calls=%async_computation | async-start | bytes 4194304 | tf_op jit(solution)/shard_map/all_to_all | solution.py:21
  24.7 63.2 %copy-start.1 = (s32[8,42]{1,0:T(8,128)}, s32[8,42]{1,0:T(8,128)S(1)}, u32[]{:S(2)}) copy-start(s32[8,42]{1,0:T(8,128)S(1)} %fusion.57) | copy-start | bytes 4036
  141.9 13.7 %copy-start.2 = (s32[8,42]{1,0:T(8,128)S(1)}, s32[8,42]{1,0:T(8,128)}, u32[]{:S(2)}) copy-start(s32[8,42]{1,0:T(8,128)} %get-tuple-element.981) | copy-start | bytes 4036
  146.0 58.5 %all-to-all-start.1 = ((bf16[32,1,1,2,128,128]{4,5,3,2,1,0:T(8,128)(2,1)}), bf16[32,1,1,2,128,128]{4,5,3,2,1,0:T(8,128)(2,1)S(1)}, u32[]{:S(2)}, u32[]{:S(2)}) async-start(bf16[32,1,1,2,128,128]{4,5,3,2,1,0:T(8,128)(2,1)} %broadcast_in_dim.207), calls=%async_computation.1 | async-start | bytes 4194304 | tf_op jit(solution)/shard_map/all_to_all | solution.py:21
Sparse Core Ops, SparseCore 0:
  9.8 67.4 all-gather.1
where the time goes:
time: 270 us; the launch traced here: 269 us
  local copies, waits for them, and re-layouts  93.6 us (35%)
  waiting for transfers between devices  92.3 us (34%)
  matrix products  38.2 us (14%)
  starting transfers between devices  21.5 us (8%)
  between operations  14.2 us (5%)
  other arithmetic  8.6 us (3%)
    gather x8, local copies, waits for them, and re-layouts, accumulate(): left_part = jnp.take(padded, picked, axis=0)  58.1 us
    all_gather x1, waiting for transfers between devices, local(): panel_all = lax.all_gather(x_blocks, 'row', axis=0, tiled=True)  48.9 us
    all_to_all x2, waiting for transfers between devices, copy_for_each(): lax.all_to_all(jnp.broadcast_to(array[None], (length, *array.shape)), axi...  42.7 us
    dot_general x8, matrix products, accumulate(): jnp.einsum('nrxy,njyz->rjxz', left_part, placed, preferred_element_type=j...  38.2 us
    all_to_all x2, starting transfers between devices, copy_for_each(): lax.all_to_all(jnp.broadcast_to(array[None], (length, *array.shape)), axi...  21.4 us
    concatenate x1, local copies, waits for them, and re-layouts, local(): jnp.concatenate([stacked, jnp.zeros((1, block_size, block_size), stacked....  10.6 us
  transfers between devices with their start and end apart: 3, of which 2 were waited for; matrix products, arithmetic and copies ran while one was open for 9% of the time, Pallas kernels for 0%

commit v1 on v0

v1 whole, which is shorter than its diff:
```python
import jax
import jax.numpy as jnp
from jax import lax
from jax.experimental import pallas as pl
from jax.experimental.pallas import tpu as pltpu
from jax.sharding import PartitionSpec as P

RB = 8
JW = 2
KB = 32
NY, NX, NZ = 4, 4, 8
CAPX = 42
TAB = 2 * 8 * 4 * 4
MESH = pl.DeviceIdType.MESH
F32 = jnp.float32
BF16 = jnp.bfloat16


def spread(core, z):
    half = z // 4
    z2 = z % 4
    e = (core + half) % 2
    dz = (1 - e) * (z2 // 2 * 2 - 1) + e * (((z2 + 1) // 2 - 1) * 2)
    return half, (z + dz + NZ) % NZ


def unspread(core, zl):
    w = (zl - 4 * core + NZ) % NZ
    z2 = (w // 2 + 1) % 4
    e = (w + 1) // 2 % 2
    return (core + e) % 2, z2


def kernel(
    tab, x_hbm, sq_ref, out_ref,
    xs, g, acc, sown, dsend, drecv, ysend, yrecv,
    xsem, s1s, s1r, zs, zr, ds, dr, ys, yr,
):
    me_r = lax.axis_index("row")
    me_c = lax.axis_index("col")
    y, k = me_r // 2, me_r % 2
    x, z = me_c // NZ, me_c % NZ
    half, zland = spread(k, z)
    kin, z2in = unspread(k, z)

    x_copy = pltpu.make_async_copy(x_hbm, xs.at[pl.ds(0, CAPX)], xsem)
    x_copy.start()

    targets = [(2 * x + half, xt * NZ + zland) for xt in range(NX)]
    sources = [(2 * yt + kin, y * NZ + 4 * k + z2in) for yt in range(NY)]
    zplus = (me_r, x * NZ + (z + 1) % NZ)
    zminus = (me_r, x * NZ + (z + NZ - 1) % NZ)
    partner = (2 * y + 1 - k, me_c)
    ypeers = [(2 * ((y + d) % NY) + k, me_c) for d in range(1, NY)]

    barrier = pltpu.get_barrier_semaphore()
    everyone = targets + sources + [zplus, zminus, partner] + ypeers
    for peer in everyone:
        pl.semaphore_signal(barrier, inc=1, device_id=peer, device_id_type=MESH)

    xs[CAPX] = jnp.zeros((128, 128), BF16)
    pl.semaphore_wait(barrier, len(everyone))

    pending = []

    def send(src, dst, ssem, rsem, peer):
        copy = pltpu.make_async_remote_copy(
            src_ref=src, dst_ref=dst, send_sem=ssem, recv_sem=rsem,
            device_id=peer, device_id_type=MESH,
        )
        copy.start()
        pending.append(copy)

    def got(dst, ssem, rsem, peer):
        pltpu.make_async_remote_copy(
            src_ref=dst, dst_ref=dst, send_sem=ssem, recv_sem=rsem,
            device_id=peer, device_id_type=MESH,
        ).wait_recv()

    def phase(ph, own_src):
        for xt in range(NX):
            send(own_src, g.at[ph, zland, y], s1s.at[ph, xt], s1r.at[ph, y], targets[xt])
        for r in range(8):
            acc[r] = jnp.zeros((256, 128), F32)

        def forward(step, way, yi):
            group = (z + NZ - step) % NZ if way == 0 else (z + step) % NZ
            part = g.at[ph, group, yi]
            send(part, part, zs.at[ph, way, step, yi], zr.at[ph, way, step, yi], zplus if way == 0 else zminus)

        def ring_got(step, way, yi):
            group = (z + 2 * NZ - step - 1) % NZ if way == 0 else (z + step + 1) % NZ
            got(g.at[ph, group, yi], zs.at[ph, way, step, yi], zr.at[ph, way, step, yi], zplus if way == 0 else zminus)

        def multiply(zl):
            ksrc, z2 = unspread(k, zl)

            def one(yi, carry):
                r = 2 * yi + ksrc
                base = ((ph * 8 + r) * 4 + z2) * 4
                b = [xs[tab[base + i]] for i in range(4)]
                left = jnp.concatenate(
                    [jnp.concatenate([b[0], b[1]], axis=1), jnp.concatenate([b[2], b[3]], axis=1)], axis=0
                )
                right = g[ph, zl, yi].reshape(256, 128)
                acc[r] += jnp.dot(left, right, preferred_element_type=F32)
                return carry

            lax.fori_loop(0, NY, one, 0)

        for yi in range(NY):
            got(g.at[ph, z, yi], s1s.at[ph, 0], s1r.at[ph, yi], targets[0])
            forward(0, 0, yi)
            forward(0, 1, yi)
        if ph == 0:
            x_copy.wait()
        multiply(z)
        for step in range(4):
            for yi in range(NY):
                if step < 3:
                    ring_got(step, 0, yi)
                    if step + 1 < 3 or yi < 2:
                        forward(step + 1, 0, yi)
                    ring_got(step, 1, yi)
                    if step + 1 < 3 or yi >= 2:
                        forward(step + 1, 1, yi)
                else:
                    ring_got(step, 0 if yi < 2 else 1, yi)
            multiply((z + NZ - step - 1) % NZ)
            if step < 3:
                multiply((z + step + 1) % NZ)

        for yi in range(NY):
            dsend[ph, yi] = acc[2 * yi + 1 - k].astype(BF16)
        send(dsend.at[ph], drecv.at[ph], ds.at[ph], dr.at[ph], partner)
        got(drecv.at[ph], ds.at[ph], dr.at[ph], partner)
        for d in range(1, NY):
            yt = (y + d) % NY
            ysend[ph, d - 1] = (acc[2 * yt + k] + drecv[ph, yt].astype(F32)).astype(BF16)
            send(ysend.at[ph, d - 1], yrecv.at[ph, d - 1], ys.at[ph, d - 1], yr.at[ph, d - 1], ypeers[d - 1])
        total = acc[2 * y + k] + drecv[ph, y].astype(F32)
        for d in range(1, NY):
            got(yrecv.at[ph, d - 1], ys.at[ph, d - 1], yr.at[ph, d - 1], ypeers[d - 1])
            total = total + yrecv[ph, d - 1].astype(F32)
        return total.reshape(2, 128, 128)

    count = tab[TAB + 2]
    square = phase(0, x_hbm.at[pl.ds(0, 2)])
    for t in range(2):
        block = jnp.where(count > t, square[t], 0.0).astype(BF16)
        sown[t] = block
        sq_ref[t] = block
    second = phase(1, sown)
    for t in range(2):
        mixed = 1.5 * xs[tab[TAB + t]].astype(F32) - 0.5 * second[t]
        out_ref[t] = jnp.where(count > t, mixed, 0.0).astype(BF16)
    for copy in pending:
        copy.wait_send()


def local(x_blocks, x_slots, x_count, s_slots, s_count):
    row = lax.axis_index("row")
    col = lax.axis_index("col")
    ordinal = jnp.arange(CAPX, dtype=jnp.int32)
    own = lax.dynamic_slice(x_slots, (row, col, 0), (1, 1, CAPX)).reshape(CAPX)
    own_count = lax.dynamic_slice(x_count, (row, col), (1, 1)).reshape(())
    own = jnp.where(ordinal < own_count, own, -2)
    so = lax.dynamic_slice(s_slots, (0, col, 0), (8, 1, 2))[:, None, 0, :, None]
    lane = jnp.arange(2, dtype=jnp.int32)
    z2 = jnp.arange(4, dtype=jnp.int32)[None, :, None, None]

    def wanted(slots, count, stride):
        at = lax.dynamic_slice(slots, (0, 4 * row, 0), (8, 4, 2))[:, :, None, :]
        live = lane < lax.dynamic_slice(count, (0, 4 * row), (8, 4))[:, :, None, None]
        ok = live & (at % stride == so % JW)
        return jnp.where(ok, so // JW * KB + z2 * RB + at // stride, -1).reshape(-1)

    mine = lax.dynamic_slice(s_slots, (row, col, 0), (1, 1, 2)).reshape(2)
    targets = jnp.concatenate(
        [wanted(x_slots, x_count, KB), wanted(s_slots, s_count, JW), mine // JW * KB + mine % JW]
    )
    found = CAPX + jnp.sum(jnp.where(targets[:, None] == own, ordinal - CAPX, 0), axis=1)
    count = lax.dynamic_slice(s_count, (row, col), (1, 1)).reshape(1)
    tab = jnp.concatenate([found, count])
    dma = pltpu.SemaphoreType.DMA
    part = jax.ShapeDtypeStruct((2, 128, 128), BF16)
    vmem = pl.BlockSpec(memory_space=pltpu.VMEM)
    square, result = pl.pallas_call(
        kernel,
        out_shape=(part, part),
        in_specs=[pl.BlockSpec(memory_space=pltpu.SMEM), pl.BlockSpec(memory_space=pl.ANY)],
        out_specs=(vmem, vmem),
        scratch_shapes=[
            pltpu.VMEM((CAPX + 1, 128, 128), BF16),
            pltpu.VMEM((2, NZ, NY, 2, 128, 128), BF16),
            pltpu.VMEM((8, 256, 128), F32),
            pltpu.VMEM((2, 128, 128), BF16),
            pltpu.VMEM((2, NY, 256, 128), BF16),
            pltpu.VMEM((2, NY, 256, 128), BF16),
            pltpu.VMEM((2, NY - 1, 256, 128), BF16),
            pltpu.VMEM((2, NY - 1, 256, 128), BF16),
            dma,
            dma((2, NX)), dma((2, NY)),
            dma((2, 2, 4, NY)), dma((2, 2, 4, NY)),
            dma((2,)), dma((2,)),
            dma((2, NY - 1)), dma((2, NY - 1)),
        ],
        compiler_params=pltpu.CompilerParams(collective_id=0, has_side_effects=True),
    )(tab, x_blocks.reshape(CAPX, 128, 128))
    return square[None, None], result[None, None]


def solution(mesh):
    in_specs = (P("row", "col", None, None, None), P(), P(), P(), P())
    out_specs = (P("row", "col", None, None, None), P("row", "col", None, None, None))
    return jax.shard_map(local, mesh=mesh, in_specs=in_specs, out_specs=out_specs, check_vma=False)
```

time: 270 us -> 103 us (0.38)
  waiting for transfers between devices: 92.3 us -> 0 us
  Pallas kernels: 0 us -> 88.4 us
  local copies, waits for them, and re-layouts: 93.6 us -> 9.89 us
  matrix products: 38.2 us -> 0 us
  starting transfers between devices: 21.5 us -> 0 us
  between operations: 14.2 us -> 0.7 us
  other arithmetic: 8.6 us -> 3.96 us
    pallas_call x0 -> x1, Pallas kernels: none -> 88.4 us  [local(): pl.pallas_call(kernel, out_shape=(part, part), in_specs=[pl.BlockSpec(mem...]
    gather x11 -> x0, local copies, waits for them, and re-layouts: 64 us -> none  [the longest x8 58.1 us: accumulate(): left_part = jnp.take(padded, picked, axis=0)]
    all_gather x1 -> x0, waiting for transfers between devices: 48.9 us -> none  [local(): panel_all = lax.all_gather(x_blocks, 'row', axis=0, tiled=True)]
    all_to_all x2 -> x0, waiting for transfers between devices: 42.7 us -> none  [copy_for_each(): lax.all_to_all(jnp.broadcast_to(array[None], (length, *array.shape)), axi...]
    dot_general x8 -> x0, matrix products: 38.2 us -> none  [accumulate(): jnp.einsum('nrxy,njyz->rjxz', left_part, placed, preferred_element_type=j...]
    all_to_all x2 -> x0, starting transfers between devices: 21.4 us -> none  [copy_for_each(): lax.all_to_all(jnp.broadcast_to(array[None], (length, *array.shape)), axi...]
    concatenate x1 -> x0, local copies, waits for them, and re-layouts: 10.6 us -> none  [local(): jnp.concatenate([stacked, jnp.zeros((1, block_size, block_size), stacked....]
    broadcast_in_dim x12 -> x0, local copies, waits for them, and re-layouts: 5.38 us -> none  [the longest x4 4.7 us: copy_for_each(): jnp.broadcast_to(array[None], (length, *array.shape))]
  transfers between devices with their start and end apart: 3 -> 0, of which waited for: 2 -> 0; matrix products, arithmetic and copies ran while one was open for 9% -> 0% of each run, Pallas kernels for 0% -> 0%
where the time goes in v1:
time: 103 us
  Pallas kernels  88.4 us (86%)
  local copies, waits for them, and re-layouts  9.89 us (10%)
  other arithmetic  3.96 us (4%)
    pallas_call x1, Pallas kernels, local(): pl.pallas_call(kernel, out_shape=(part, part), in_specs=[pl.BlockSpec(mem...  88.4 us
    unnamed x3, local copies, waits for them, and re-layouts  3.08 us

profile of v1, /device:TPU:1, one launch (start us, length us, event | category | flops | bytes accessed | tf_op | source)
XLA Modules:
  0.0 103.0 jit_solution(8921241349076013859)
XLA Ops:
  0.6 1.3 %dynamic_slice.35 = s32[1,1]{1,0:T(1,128)} dynamic-slice(s32[8,32]{1,0:T(8,128)} %param.9, s32[]{:T(128)S(6)} %select_n.116, s32[]{:T(128)S(6)} %select_n.106), dynamic_slice_sizes={1,1} | dynamic-slice | bytes 12 | tf_op jit(solution)/shard_map/dynamic_slice | solution.py:183
  1.9 1.3 %dynamic_slice.33 = s32[1,1]{1,0:T(1,128)} dynamic-slice(s32[8,32]{1,0:T(8,128)} %param.7, s32[]{:T(128)S(6)} %select_n.116, s32[]{:T(128)S(6)} %select_n.106), dynamic_slice_sizes={1,1} | dynamic-slice | bytes 12 | tf_op jit(solution)/shard_map/dynamic_slice | solution.py:166
  3.2 0.9 fusion
  4.1 1.3 %compare_select_fusion = (s32[42]{0:T(128)S(1)}, s32[42]{0:T(128)S(1)}) fusion(s32[8,32,42]{2,1,0:T(8,128)} %param.6, s32[]{:T(128)S(6)} %select_n.116, s32[]{:T(128)S(6)} %select_n.106, s32[]{:T(128)} %bitcast.1), kind=kLoop, calls=%fused_computation.22 | loop fusion | flops 126 | bytes 516 | tf_op jit(solution)/shard_map/jit(_where)/select_n | solution.py:167
  5.4 0.8 constant_dynamic-slice_fusion.3
  6.2 0.1 copy.25
  6.3 0.1 copy.26
  6.4 0.1 copy.27
  6.5 0.8 constant_dynamic-slice_fusion.2
  7.5 0.8 constant_dynamic-slice_fusion.4
  8.2 0.1 copy.31
  8.4 0.1 copy.24
  8.5 0.8 and_select_fusion.3
  9.3 0.1 copy.29
  9.5 0.1 copy.30
  9.6 0.1 copy.28
  9.7 0.1 and_select_fusion.1
  9.9 0.1 select_n.111
  10.0 0.1 select_n.115
  10.2 0.1 select_reduce_fusion
  10.3 1.3 %pad_add_fusion.1.tab = s32[259]{0:T(512)} fusion(s32[1]{0:T(128)} %bitcast.3, s32[258]{0:T(512)S(1)} %broadcast_add_fusion.1), kind=kLoop, calls=%fused_computation.21 | loop fusion | flops 259 | bytes 2072 | tf_op jit(solution)/shard_map/concatenate | solution.py:184
  11.6 88.4 %shard_map.68 = (bf16[2,128,128]{2,1,0:T(8,128)(2,1)}, bf16[2,128,128]{2,1,0:T(8,128)(2,1)}) custom-call(s32[259]{0:T(512)} %pad_add_fusion.1.tab, bf16[42,128,128]{2,1,0:T(8,128)(2,1)} %bitcast.31), custom_call_target="tpu_custom_call" | custom-call | tf_op jit(solution)/shard_map/pallas_call | solution.py:188
  100.0 1.5 %copy.34 = bf16[1,1,2,128,128]{4,3,2,1,0:T(8,128)(2,1)} copy(bf16[1,1,2,128,128]{4,3,2,1,0:T(8,128)(2,1)} %bitcast.33) | data formatting | bytes 131072
  101.5 1.5 %copy.35 = bf16[1,1,2,128,128]{4,3,2,1,0:T(8,128)(2,1)} copy(bf16[1,1,2,128,128]{4,3,2,1,0:T(8,128)(2,1)} %bitcast.32) | data formatting | bytes 131072
  (9 shorter events, 0.3 us)

commit v2 on v1

v2 whole, which is shorter than its diff:
```python
import jax
import jax.numpy as jnp
from jax import lax
from jax.experimental import pallas as pl
from jax.experimental.pallas import tpu as pltpu
from jax.sharding import PartitionSpec as P

RB = 8
JW = 2
KB = 32
NY, NX, NZ = 4, 4, 8
CAPX = 42
MESH = pl.DeviceIdType.MESH
F32 = jnp.float32
BF16 = jnp.bfloat16
I32 = jnp.int32


def spread(core, z):
    half = z // 4
    z2 = z % 4
    e = (core + half) % 2
    dz = (1 - e) * (z2 // 2 * 2 - 1) + e * (((z2 + 1) // 2 - 1) * 2)
    return half, (z + dz + NZ) % NZ


def unspread(core, zl):
    w = (zl - 4 * core + NZ) % NZ
    z2 = (w // 2 + 1) % 4
    e = (w + 1) // 2 % 2
    return (core + e) % 2, z2


def find_blocks(me_r, me_c, x_slots, x_count, s_slots, s_count, tabv):
    lane = lax.broadcasted_iota(I32, (8, 128), 1)
    lane32 = lax.broadcasted_iota(I32, (8, 32), 1)

    def column(values, at):
        return jnp.sum(jnp.where(lane32 == at, values, 0), axis=1, keepdims=True)

    rows = [s_slots[:, t, :] for t in range(2)]
    xc, sc = x_count[...], s_count[...]
    so = [column(rows[t], me_c) for t in range(2)]
    bit = lane // 2 % 2
    so_lane = jnp.where(bit == 0, so[0], so[1])
    at_row = jnp.zeros((8, 128), I32)
    at_col = jnp.zeros((8, 128), I32)
    live = jnp.zeros((8, 128), I32)
    for z2 in range(4):
        c = 4 * me_r + z2
        near = x_slots[:, c, :]
        counts = (column(xc, c), column(sc, c))
        for n in range(2):
            px = near[:, n : n + 1]
            ps = column(rows[n], c)
            for ph, p, stride in ((0, px, KB), (1, ps, JW)):
                here = (lane // 4 == ph * 4 + z2) & (lane % 2 == n)
                at_row = jnp.where(here, z2 * RB + p // stride, at_row)
                at_col = jnp.where(here, p % stride, at_col)
                live = jnp.where(here, jnp.where(counts[ph] > n, 1, 0), live)
    want = jnp.where((live == 1) & (at_col == so_lane % JW), so_lane // JW * KB + at_row, -1)
    for t in range(2):
        want = jnp.where(lane == 32 + t, so[t] // JW * KB + so[t] % JW, want)
    own = x_slots[me_r, pl.ds(me_c, 1), :]
    own_count = jnp.sum(jnp.where(lane32[:1] == me_c, x_count[pl.ds(me_r, 1), :], 0), axis=1, keepdims=True)
    own = jnp.where(lax.broadcasted_iota(I32, (1, CAPX), 1) < own_count, own, -2)
    found = jnp.full((8, 128), CAPX, I32)
    for s in range(CAPX):
        found = jnp.where(want == own[:, s : s + 1], s, found)
    tabv[...] = jnp.where(lane == 34, column(sc, me_c), found)


def kernel(
    x_slots, x_count, s_slots, s_count, x_hbm, out_ref,
    xs, g, acc, sown, drecv, ysend, yrecv, tabv, tab,
    xsem, tsem, as_, ar, bs, br, zas, zar, zbs, zbr, xbs, xbr, ds, dr, ys, yr,
):
    me_r = lax.axis_index("row")
    me_c = lax.axis_index("col")
    y, k = me_r // 2, me_r % 2
    x, z = me_c // NZ, me_c % NZ
    half, zland = spread(k, z)
    kin, z2in = unspread(k, z)

    x_copy = pltpu.make_async_copy(x_hbm, xs.at[pl.ds(0, CAPX)], xsem)
    x_copy.start()

    targets = [(2 * x + half, xt * NZ + zland) for xt in range(NX)]
    landing = (2 * x + half, y * NZ + zland)
    sources = [(2 * yt + kin, y * NZ + 4 * k + z2in) for yt in range(NY)]
    zpeer = [(me_r, x * NZ + (z + 1) % NZ), (me_r, x * NZ + (z + NZ - 1) % NZ)]
    partner = (2 * y + 1 - k, me_c)
    ypeer = [(2 * ((y + d) % NY) + k, me_c) for d in range(1, NY)]

    def xpeer(dx):
        return (me_r, (x + dx + NX) % NX * NZ + z)

    barrier = pltpu.get_barrier_semaphore()
    everyone = targets + sources + zpeer + [partner] + ypeer + [xpeer(1), xpeer(-1)]
    for peer in everyone:
        pl.semaphore_signal(barrier, inc=1, device_id=peer, device_id_type=MESH)
    xs[CAPX] = jnp.zeros((128, 128), BF16)
    pl.semaphore_wait(barrier, len(everyone))

    pending = []

    def remote(src, dst, sems, peer):
        return pltpu.make_async_remote_copy(
            src_ref=src, dst_ref=dst, send_sem=sems[0], recv_sem=sems[1],
            device_id=peer, device_id_type=MESH,
        )

    def send(src, dst, sems, peer):
        copy = remote(src, dst, sems, peer)
        copy.start()
        pending.append(copy)

    def got(dst, sems, peer):
        remote(dst, dst, sems, peer).wait_recv()

    def phase(ph, own_a, own_b):
        def block(zl, yi, n):
            return g.at[ph, zl, yi, n]

        send(own_b, block(zland, y, 1), (bs.at[ph], br.at[ph]), landing)
        for d in range(NX):
            xt = (x + d + 1) % NX
            peer = (2 * x + half, xt * NZ + zland)
            send(own_a, block(zland, y, 0), (as_.at[ph, d], ar.at[ph, y]), peer)

        if ph == 0:
            find_blocks(me_r, me_c, x_slots, x_count, s_slots, s_count, tabv)
            tab_copy = pltpu.make_async_copy(tabv, tab, tsem)
            tab_copy.start()
        for r in range(8):
            acc[ph, r] = jnp.zeros((256, 128), F32)
        if ph == 0:
            tab_copy.wait()
            x_copy.wait()

        def sign(zl):
            return 1 - 2 * (zl % 2)

        def xsems(slot, zl):
            return (xbs.at[ph, slot, zl], xbr.at[ph, slot, zl])

        def group(step, way):
            return (z + NZ - step) % NZ if way == 0 else (z + step) % NZ

        def ring(step, way, yi):
            zl = group(step, way)
            send(block(zl, yi, 0), block(zl, yi, 0), (zas.at[ph, way, step, yi], zar.at[ph, way, step, yi]), zpeer[way])

        def ring_got(step, way, yi):
            got(block(group(step + 1, way), yi, 0), (zas.at[ph, way, step, yi], zar.at[ph, way, step, yi]), zpeer[way])

        def ring_b(step, way):
            zl = group(step, way)
            send(block(zl, x, 1), block(zl, x, 1), (zbs.at[ph, way, step], zbr.at[ph, way, step]), zpeer[way])

        def ring_b_got(step, way):
            got(block(group(step + 1, way), x, 1), (zbs.at[ph, way, step], zbr.at[ph, way, step]), zpeer[way])

        def cast(zl):
            for slot, dx in ((0, sign(zl)), (1, -sign(zl))):
                send(block(zl, x, 1), block(zl, x, 1), xsems(slot, zl), xpeer(dx))

        def relay(zl):
            part = block(zl, (x - sign(zl) + NX) % NX, 1)
            got(part, xsems(0, zl), xpeer(1))
            send(part, part, xsems(2, zl), xpeer(sign(zl)))

        def multiply(zl):
            got(block(zl, (x + sign(zl) + NX) % NX, 1), xsems(1, zl), xpeer(1))
            got(block(zl, (x + 2) % NX, 1), xsems(2, zl), xpeer(1))
            ksrc, z2 = unspread(k, zl)

            def one(yi, carry):
                r = 2 * yi + ksrc
                base = (ph * 4 + z2) * 4
                b = [xs[tab[r, base + i]] for i in range(4)]
                left = jnp.concatenate(
                    [jnp.concatenate([b[0], b[1]], axis=1), jnp.concatenate([b[2], b[3]], axis=1)], axis=0
                )
                right = g[ph, zl, yi].reshape(256, 128)
                acc[ph, r] += jnp.dot(left, right, preferred_element_type=F32)
                return carry

            lax.fori_loop(0, NY, one, 0)

        got(block(z, x, 1), (bs.at[ph], br.at[ph]), partner)
        ring_b(0, 0)
        ring_b(0, 1)
        cast(z)
        for yi in range(NY):
            got(block(z, yi, 0), (as_.at[ph, 0], ar.at[ph, yi]), partner)
            ring(0, 0, yi)
            ring(0, 1, yi)
        arrived = [[z]] + [[group(s, 0), group(s, 1)] for s in range(1, 4)] + [[group(4, 0)]]
        for step in range(4):
            last = step == 3
            for way in range(1 if last else 2):
                ring_b_got(step, way)
                if step < 2 or (step == 2 and way == 0):
                    ring_b(step + 1, way)
                cast(group(step + 1, way))
            for zl in arrived[step]:
                relay(zl)
            for yi in range(NY):
                for way in range(2):
                    if last and way != yi // 2:
                        continue
                    ring_got(step, way, yi)
                    if step < 2 or (step == 2 and way == yi // 2):
                        ring(step + 1, way, yi)
            if step >= 1:
                for zl in arrived[step - 1]:
                    multiply(zl)
        for zl in arrived[4]:
            relay(zl)
        for zl in arrived[3] + arrived[4]:
            multiply(zl)

        for yi in range(NY):
            send(acc.at[ph, 2 * yi + 1 - k], drecv.at[ph, yi], (ds.at[ph, yi], dr.at[ph, yi]), partner)
        for yi in range(NY):
            got(drecv.at[ph, yi], (ds.at[ph, yi], dr.at[ph, yi]), partner)
        for d in (2, 1, 3):
            yt = (y + d) % NY
            ysend[ph, d - 1] = (acc[ph, 2 * yt + k] + drecv[ph, yt]).astype(BF16)
            send(ysend.at[ph, d - 1], yrecv.at[ph, d - 1], (ys.at[ph, d - 1], yr.at[ph, d - 1]), ypeer[d - 1])
        total = acc[ph, 2 * y + k] + drecv[ph, y]
        for d in (1, 3, 2):
            got(yrecv.at[ph, d - 1], (ys.at[ph, d - 1], yr.at[ph, d - 1]), ypeer[d - 1])
            total = total + yrecv[ph, d - 1].astype(F32)
        return total.reshape(2, 128, 128)

    square = phase(0, x_hbm.at[0], x_hbm.at[1])
    count = tab[me_r, 34]
    for t in range(2):
        block = jnp.where(count > t, square[t], 0.0).astype(BF16)
        sown[t] = block
        out_ref[t] = block
    second = phase(1, sown.at[0], sown.at[1])
    for t in range(2):
        mixed = 1.5 * xs[tab[me_r, 32 + t]].astype(F32) - 0.5 * second[t]
        out_ref[2 + t] = jnp.where(count > t, mixed, 0.0).astype(BF16)
    for copy in pending:
        copy.wait_send()


def split(both, square, result):
    square[...] = both[:2]
    result[...] = both[2:]


def local(x_blocks, x_slots, x_count, s_slots, s_count):
    dma = pltpu.SemaphoreType.DMA
    vmem = pl.BlockSpec(memory_space=pltpu.VMEM)
    both = pl.pallas_call(
        kernel,
        out_shape=jax.ShapeDtypeStruct((4, 128, 128), BF16),
        in_specs=[vmem] * 4 + [pl.BlockSpec(memory_space=pl.ANY)],
        out_specs=vmem,
        scratch_shapes=[
            pltpu.VMEM((CAPX + 1, 128, 128), BF16),
            pltpu.VMEM((2, NZ, NY, 2, 128, 128), BF16),
            pltpu.VMEM((2, 8, 256, 128), F32),
            pltpu.VMEM((2, 128, 128), BF16),
            pltpu.VMEM((2, NY, 256, 128), F32),
            pltpu.VMEM((2, NY - 1, 256, 128), BF16),
            pltpu.VMEM((2, NY - 1, 256, 128), BF16),
            pltpu.VMEM((8, 128), I32),
            pltpu.SMEM((8, 128), I32),
            dma, dma,
            dma((2, NX)), dma((2, NY)),
            dma((2,)), dma((2,)),
            dma((2, 2, 4, NY)), dma((2, 2, 4, NY)),
            dma((2, 2, 4)), dma((2, 2, 4)),
            dma((2, 3, NZ)), dma((2, 3, NZ)),
            dma((2, NY)), dma((2, NY)),
            dma((2, NY - 1)), dma((2, NY - 1)),
        ],
        compiler_params=pltpu.CompilerParams(collective_id=0, has_side_effects=True),
    )(x_slots, x_count, s_slots.transpose(0, 2, 1), s_count, x_blocks.reshape(CAPX, 128, 128))
    part = jax.ShapeDtypeStruct((2, 128, 128), BF16)
    square, result = pl.pallas_call(
        split, out_shape=(part, part), in_specs=[vmem], out_specs=(vmem, vmem)
    )(both)
    return square[None, None], result[None, None]


def solution(mesh):
    in_specs = (P("row", "col", None, None, None), P(), P(), P(), P())
    out_specs = (P("row", "col", None, None, None), P("row", "col", None, None, None))
    return jax.shard_map(local, mesh=mesh, in_specs=in_specs, out_specs=out_specs, check_vma=False)
```

time: 103 us -> 86.3 us (0.84)
  local copies, waits for them, and re-layouts: 9.89 us -> 0 us
  other arithmetic: 3.96 us -> 0 us
  Pallas kernels: 88.4 us -> 85.6 us
    dynamic_slice x7 -> x0, local copies, waits for them, and re-layouts: 5.82 us -> none  [the longest x1 1.28 us: local(): count = lax.dynamic_slice(s_count, (row, col), (1, 1)).reshape(1)]
    unnamed x3 -> x0, local copies, waits for them, and re-layouts: 3.08 us -> none
    pallas_call x1 -> x2, Pallas kernels: 88.4 us -> 85.6 us  [the longest x1 84 us: local(): pl.pallas_call(kernel, out_shape=jax.ShapeDtypeStruct((4, 128, 128), BF16...]
    select_n x5 -> x0, other arithmetic: 2.31 us -> none  [the longest x1 1.34 us: local(): own = jnp.where(ordinal < own_count, own, -2)]
    concatenate x2 -> x0, other arithmetic: 1.31 us -> none  [the longest x1 1.3 us: local(): tab = jnp.concatenate([found, count])]
where the time goes in v2:
time: 86.3 us; the launch traced here: 86.2 us
  Pallas kernels  85.6 us (99%)
    pallas_call x1, Pallas kernels, local(): pl.pallas_call(kernel, out_shape=jax.ShapeDtypeStruct((4, 128, 128), BF16...  84 us

profile of v2, /device:TPU:1, one launch (start us, length us, event | category | flops | bytes accessed | tf_op | source)
XLA Modules:
  0.0 86.2 jit_solution(16770650278827347298)
XLA Ops:
  0.6 84.0 %shard_map.68.both = bf16[4,128,128]{2,1,0:T(8,128)(2,1)} custom-call(s32[8,32,42]{2,1,0:T(8,128)} %x_slots.1, s32[8,32]{1,0:T(8,128)} %x_count.1, s32[8,2,32]{2,1,0:T(2,128)} %bitcast.5, s32[8,32]{1,0:T(8,128)} %s_count.1, bf16[42,128,128]{2,1,0:T(8,128)(2,1)} %bitcast.4), custom_call_target="tpu_custom_call" | custom-call | tf_op jit(solution)/shard_map/pallas_call | solution.py:260
  84.6 1.6 %shard_map.69 = (bf16[2,128,128]{2,1,0:T(8,128)(2,1)}, bf16[2,128,128]{2,1,0:T(8,128)(2,1)}) custom-call(bf16[4,128,128]{2,1,0:T(8,128)(2,1)} %shard_map.68.both), custom_call_target="tpu_custom_call" | custom-call | tf_op jit(solution)/shard_map/pallas_call | solution.py:287

commit v3 on v2

--- a/solution.py
+++ b/solution.py
@@ -71,9 +71,9 @@
 
 
 def kernel(
-    x_slots, x_count, s_slots, s_count, x_hbm, out_ref,
-    xs, g, acc, sown, drecv, ysend, yrecv, tabv, tab,
-    xsem, tsem, as_, ar, bs, br, zas, zar, zbs, zbr, xbs, xbr, ds, dr, ys, yr,
+    x_slots_hbm, x_count_hbm, s_slots_hbm, s_count_hbm, x_hbm, out_ref,
+    x_slots, x_count, s_slots, s_count, xs, g, acc, sown, drecv, ysend, yrecv, tabv, tab,
+    xsem, tsem, isem, as_, ar, bs, br, zas, zar, zbs, zbr, xbs, xbr, ds, dr, ys, yr,
 ):
     me_r = lax.axis_index("row")
     me_c = lax.axis_index("col")
@@ -82,13 +82,10 @@
     half, zland = spread(k, z)
     kin, z2in = unspread(k, z)
 
-    x_copy = pltpu.make_async_copy(x_hbm, xs.at[pl.ds(0, CAPX)], xsem)
-    x_copy.start()
-
     targets = [(2 * x + half, xt * NZ + zland) for xt in range(NX)]
     landing = (2 * x + half, y * NZ + zland)
     sources = [(2 * yt + kin, y * NZ + 4 * k + z2in) for yt in range(NY)]
-    zpeer = [(me_r, x * NZ + (z + 1) % NZ), (me_r, x * NZ + (z + NZ - 1) % NZ)]
+    zpeer = [(me_r, x * NZ + (z + d + NZ) % NZ) for d in (1, -1, 2, -2)]
     partner = (2 * y + 1 - k, me_c)
     ypeer = [(2 * ((y + d) % NY) + k, me_c) for d in range(1, NY)]
 
@@ -96,9 +93,18 @@
         return (me_r, (x + dx + NX) % NX * NZ + z)
 
     barrier = pltpu.get_barrier_semaphore()
-    everyone = targets + sources + zpeer + [partner] + ypeer + [xpeer(1), xpeer(-1)]
+    everyone = targets + sources + zpeer + [partner] + ypeer + [xpeer(1), xpeer(-1), xpeer(2)]
     for peer in everyone:
         pl.semaphore_signal(barrier, inc=1, device_id=peer, device_id_type=MESH)
+    inputs = [
+        pltpu.make_async_copy(a, b, isem.at[i])
+        for i, (a, b) in enumerate(
+            [(x_slots_hbm, x_slots), (x_count_hbm, x_count), (s_slots_hbm, s_slots), (s_count_hbm, s_count)]
+        )
+    ]
+    x_copy = pltpu.make_async_copy(x_hbm, xs.at[pl.ds(0, CAPX)], xsem)
+    for copy in inputs + [x_copy]:
+        copy.start()
     xs[CAPX] = jnp.zeros((128, 128), BF16)
     pl.semaphore_wait(barrier, len(everyone))
 
@@ -129,6 +135,8 @@
             send(own_a, block(zland, y, 0), (as_.at[ph, d], ar.at[ph, y]), peer)
 
         if ph == 0:
+            for copy in inputs:
+                copy.wait()
             find_blocks(me_r, me_c, x_slots, x_count, s_slots, s_count, tabv)
             tab_copy = pltpu.make_async_copy(tabv, tab, tsem)
             tab_copy.start()
@@ -154,23 +162,27 @@
         def ring_got(step, way, yi):
             got(block(group(step + 1, way), yi, 0), (zas.at[ph, way, step, yi], zar.at[ph, way, step, yi]), zpeer[way])
 
-        def ring_b(step, way):
-            zl = group(step, way)
-            send(block(zl, x, 1), block(zl, x, 1), (zbs.at[ph, way, step], zbr.at[ph, way, step]), zpeer[way])
-
-        def ring_b_got(step, way):
-            got(block(group(step + 1, way), x, 1), (zbs.at[ph, way, step], zbr.at[ph, way, step]), zpeer[way])
-
-        def cast(zl):
-            for slot, dx in ((0, sign(zl)), (1, -sign(zl))):
-                send(block(zl, x, 1), block(zl, x, 1), xsems(slot, zl), xpeer(dx))
+        def send_b(zl, peer, at, rows=128, first=0):
+            part = g.at[ph, zl, x, 1, pl.ds(first, rows)]
+            send(part, part, (zbs.at[ph, at], zbr.at[ph, at]), zpeer[peer])
+
+        def got_b(zl, at, rows=128, first=0):
+            got(g.at[ph, zl, x, 1, pl.ds(first, rows)], (zbs.at[ph, at], zbr.at[ph, at]), zpeer[0])
+
+        def cast(zl, direct=False):
+            part = block(zl, x, 1)
+            for slot, dx in ((2, 2), (0, sign(zl)), (1, -sign(zl))):
+                if slot < 2 or direct:
+                    send(part, part, xsems(slot, zl), xpeer(dx))
 
         def relay(zl):
             part = block(zl, (x - sign(zl) + NX) % NX, 1)
             got(part, xsems(0, zl), xpeer(1))
             send(part, part, xsems(2, zl), xpeer(sign(zl)))
 
-        def multiply(zl):
+        def multiply(zl, direct=False):
+            if direct:
+                got(block(zl, (x - sign(zl) + NX) % NX, 1), xsems(0, zl), xpeer(1))
             got(block(zl, (x + sign(zl) + NX) % NX, 1), xsems(1, zl), xpeer(1))
             got(block(zl, (x + 2) % NX, 1), xsems(2, zl), xpeer(1))
             ksrc, z2 = unspread(k, zl)
@@ -188,47 +200,67 @@
 
             lax.fori_loop(0, NY, one, 0)
 
+        def near(d):
+            return (z + d + NZ) % NZ
+
         got(block(z, x, 1), (bs.at[ph], br.at[ph]), partner)
-        ring_b(0, 0)
-        ring_b(0, 1)
+        for i, d in ((2, 2), (3, -2), (0, 1), (1, -1)):
+            send_b(z, i, i)
         cast(z)
         for yi in range(NY):
             got(block(z, yi, 0), (as_.at[ph, 0], ar.at[ph, yi]), partner)
             ring(0, 0, yi)
             ring(0, 1, yi)
-        arrived = [[z]] + [[group(s, 0), group(s, 1)] for s in range(1, 4)] + [[group(4, 0)]]
-        for step in range(4):
-            last = step == 3
-            for way in range(1 if last else 2):
-                ring_b_got(step, way)
-                if step < 2 or (step == 2 and way == 0):
-                    ring_b(step + 1, way)
-                cast(group(step + 1, way))
-            for zl in arrived[step]:
-                relay(zl)
+        for i, d in ((0, -1), (1, 1)):
+            got_b(near(d), i)
+            cast(near(d))
+        for i, d in ((2, -2), (3, 2)):
+            got_b(near(d), i)
+            send_b(near(d), i - 2, 2 + i)
+            send_b(near(d), i, 4 + i, 64, 64 * (i - 2))
+            cast(near(d))
+        relay(z)
+
+        def advance(step):
             for yi in range(NY):
                 for way in range(2):
-                    if last and way != yi // 2:
+                    if step == 3 and way != yi // 2:
                         continue
                     ring_got(step, way, yi)
                     if step < 2 or (step == 2 and way == yi // 2):
                         ring(step + 1, way, yi)
-            if step >= 1:
-                for zl in arrived[step - 1]:
-                    multiply(zl)
-        for zl in arrived[4]:
-            relay(zl)
-        for zl in arrived[3] + arrived[4]:
-            multiply(zl)
-
-        for yi in range(NY):
-            send(acc.at[ph, 2 * yi + 1 - k], drecv.at[ph, yi], (ds.at[ph, yi], dr.at[ph, yi]), partner)
-        for yi in range(NY):
-            got(drecv.at[ph, yi], (ds.at[ph, yi], dr.at[ph, yi]), partner)
-        for d in (2, 1, 3):
-            yt = (y + d) % NY
+
+        advance(0)
+        relay(near(1))
+        relay(near(-1))
+        for i, d in ((4, -3), (5, 3)):
+            got_b(near(d), i)
+            cast(near(d), True)
+        got_b(near(4), 6, 64, 0)
+        got_b(near(4), 7, 64, 64)
+        cast(near(4), True)
+        relay(near(2))
+        relay(near(-2))
+        advance(1)
+        multiply(z)
+        multiply(near(1))
+        multiply(near(-1))
+        advance(2)
+        multiply(near(2))
+        multiply(near(-2))
+        multiply(near(3), True)
+        multiply(near(-3), True)
+        advance(3)
+        multiply(near(4), True)
+
+        order = [(y + d) % NY for d in (2, 1, 3, 0)]
+        for yt in order:
+            send(acc.at[ph, 2 * yt + 1 - k], drecv.at[ph, yt], (ds.at[ph, yt], dr.at[ph, yt]), partner)
+        for d, yt in zip((2, 1, 3), order):
+            got(drecv.at[ph, yt], (ds.at[ph, yt], dr.at[ph, yt]), partner)
             ysend[ph, d - 1] = (acc[ph, 2 * yt + k] + drecv[ph, yt]).astype(BF16)
             send(ysend.at[ph, d - 1], yrecv.at[ph, d - 1], (ys.at[ph, d - 1], yr.at[ph, d - 1]), ypeer[d - 1])
+        got(drecv.at[ph, y], (ds.at[ph, y], dr.at[ph, y]), partner)
         total = acc[ph, 2 * y + k] + drecv[ph, y]
         for d in (1, 3, 2):
             got(yrecv.at[ph, d - 1], (ys.at[ph, d - 1], yr.at[ph, d - 1]), ypeer[d - 1])
@@ -260,9 +292,13 @@
     both = pl.pallas_call(
         kernel,
         out_shape=jax.ShapeDtypeStruct((4, 128, 128), BF16),
-        in_specs=[vmem] * 4 + [pl.BlockSpec(memory_space=pl.ANY)],
+        in_specs=[pl.BlockSpec(memory_space=pl.ANY)] * 5,
         out_specs=vmem,
         scratch_shapes=[
+            pltpu.VMEM((8, 32, CAPX), I32),
+            pltpu.VMEM((8, 32), I32),
+            pltpu.VMEM((8, 2, 32), I32),
+            pltpu.VMEM((8, 32), I32),
             pltpu.VMEM((CAPX + 1, 128, 128), BF16),
             pltpu.VMEM((2, NZ, NY, 2, 128, 128), BF16),
             pltpu.VMEM((2, 8, 256, 128), F32),
@@ -272,11 +308,11 @@
             pltpu.VMEM((2, NY - 1, 256, 128), BF16),
             pltpu.VMEM((8, 128), I32),
             pltpu.SMEM((8, 128), I32),
-            dma, dma,
+            dma, dma, dma((4,)),
             dma((2, NX)), dma((2, NY)),
             dma((2,)), dma((2,)),
             dma((2, 2, 4, NY)), dma((2, 2, 4, NY)),
-            dma((2, 2, 4)), dma((2, 2, 4)),
+            dma((2, 8)), dma((2, 8)),
             dma((2, 3, NZ)), dma((2, 3, NZ)),
             dma((2, NY)), dma((2, NY)),
             dma((2, NY - 1)), dma((2, NY - 1)),

time: 86.3 us -> 78.3 us (0.907)
  Pallas kernels: 85.6 us -> 77.5 us
    pallas_call x1, Pallas kernels: 84 us -> 76 us  [local(): pl.pallas_call(kernel, out_shape=jax.ShapeDtypeStruct((4, 128, 128), BF16...]
where the time goes in v3:
time: 78.3 us; the launch traced here: 78.2 us
  Pallas kernels  77.5 us (99%)
    pallas_call x1, Pallas kernels, local(): pl.pallas_call(kernel, out_shape=jax.ShapeDtypeStruct((4, 128, 128), BF16...  76 us

profile of v3, /device:TPU:1, one launch (start us, length us, event | category | flops | bytes accessed | tf_op | source)
XLA Modules:
  0.0 78.2 jit_solution(11226375508765859243)
XLA Ops:
  0.6 76.0 %shard_map.68.both = bf16[4,128,128]{2,1,0:T(8,128)(2,1)} custom-call(s32[8,32,42]{2,1,0:T(8,128)} %x_slots_hbm.1, s32[8,32]{1,0:T(8,128)} %x_count_hbm.1, s32[8,2,32]{2,1,0:T(2,128)} %bitcast.5, s32[8,32]{1,0:T(8,128)} %s_count_hbm.1, bf16[42,128,128]{2,1,0:T(8,128)(2,1)} %bitcast.4), custom_call_target="tpu_custom_call" | custom-call | tf_op jit(solution)/shard_map/pallas_call | solution.py:292
  76.6 1.6 %shard_map.69 = (bf16[2,128,128]{2,1,0:T(8,128)(2,1)}, bf16[2,128,128]{2,1,0:T(8,128)(2,1)}) custom-call(bf16[4,128,128]{2,1,0:T(8,128)(2,1)} %shard_map.68.both), custom_call_target="tpu_custom_call" | custom-call | tf_op jit(solution)/shard_map/pallas_call | solution.py:323

commit v4 on v3

--- a/solution.py
+++ b/solution.py
@@ -124,15 +124,18 @@
     def got(dst, sems, peer):
         remote(dst, dst, sems, peer).wait_recv()
 
-    def phase(ph, own_a, own_b):
+    def launch(ph, n, own):
+        part = g.at[ph, zland, y, n]
+        if n == 1:
+            send(own, part, (bs.at[ph], br.at[ph]), landing)
+            return
+        for d in range(NX):
+            peer = (2 * x + half, (x + d + 1) % NX * NZ + zland)
+            send(own, part, (as_.at[ph, d], ar.at[ph, y]), peer)
+
+    def phase(ph, finish):
         def block(zl, yi, n):
             return g.at[ph, zl, yi, n]
-
-        send(own_b, block(zland, y, 1), (bs.at[ph], br.at[ph]), landing)
-        for d in range(NX):
-            xt = (x + d + 1) % NX
-            peer = (2 * x + half, xt * NZ + zland)
-            send(own_a, block(zland, y, 0), (as_.at[ph, d], ar.at[ph, y]), peer)
 
         if ph == 0:
             for copy in inputs:
@@ -198,7 +201,7 @@
                 acc[ph, r] += jnp.dot(left, right, preferred_element_type=F32)
                 return carry
 
-            lax.fori_loop(0, NY, one, 0)
+            lax.fori_loop(0, NY, one, 0, unroll=True)
 
         def near(d):
             return (z + d + NZ) % NZ
@@ -206,20 +209,19 @@
         got(block(z, x, 1), (bs.at[ph], br.at[ph]), partner)
         for i, d in ((2, 2), (3, -2), (0, 1), (1, -1)):
             send_b(z, i, i)
-        cast(z)
+        cast(z, True)
         for yi in range(NY):
             got(block(z, yi, 0), (as_.at[ph, 0], ar.at[ph, yi]), partner)
             ring(0, 0, yi)
             ring(0, 1, yi)
         for i, d in ((0, -1), (1, 1)):
             got_b(near(d), i)
-            cast(near(d))
+            cast(near(d), True)
         for i, d in ((2, -2), (3, 2)):
             got_b(near(d), i)
             send_b(near(d), i - 2, 2 + i)
             send_b(near(d), i, 4 + i, 64, 64 * (i - 2))
-            cast(near(d))
-        relay(z)
+            cast(near(d), True)
 
         def advance(step):
             for yi in range(NY):
@@ -231,52 +233,61 @@
                         ring(step + 1, way, yi)
 
         advance(0)
-        relay(near(1))
-        relay(near(-1))
         for i, d in ((4, -3), (5, 3)):
             got_b(near(d), i)
             cast(near(d), True)
         got_b(near(4), 6, 64, 0)
         got_b(near(4), 7, 64, 64)
         cast(near(4), True)
-        relay(near(2))
-        relay(near(-2))
         advance(1)
-        multiply(z)
-        multiply(near(1))
-        multiply(near(-1))
+        multiply(z, True)
+        multiply(near(1), True)
+        multiply(near(-1), True)
         advance(2)
-        multiply(near(2))
-        multiply(near(-2))
+        multiply(near(2), True)
+        multiply(near(-2), True)
         multiply(near(3), True)
         multiply(near(-3), True)
         advance(3)
         multiply(near(4), True)
 
         order = [(y + d) % NY for d in (2, 1, 3, 0)]
-        for yt in order:
-            send(acc.at[ph, 2 * yt + 1 - k], drecv.at[ph, yt], (ds.at[ph, yt], dr.at[ph, yt]), partner)
-        for d, yt in zip((2, 1, 3), order):
-            got(drecv.at[ph, yt], (ds.at[ph, yt], dr.at[ph, yt]), partner)
-            ysend[ph, d - 1] = (acc[ph, 2 * yt + k] + drecv[ph, yt]).astype(BF16)
-            send(ysend.at[ph, d - 1], yrecv.at[ph, d - 1], (ys.at[ph, d - 1], yr.at[ph, d - 1]), ypeer[d - 1])
-        got(drecv.at[ph, y], (ds.at[ph, y], dr.at[ph, y]), partner)
-        total = acc[ph, 2 * y + k] + drecv[ph, y]
-        for d in (1, 3, 2):
-            got(yrecv.at[ph, d - 1], (ys.at[ph, d - 1], yr.at[ph, d - 1]), ypeer[d - 1])
-            total = total + yrecv[ph, d - 1].astype(F32)
-        return total.reshape(2, 128, 128)
-
-    square = phase(0, x_hbm.at[0], x_hbm.at[1])
-    count = tab[me_r, 34]
-    for t in range(2):
-        block = jnp.where(count > t, square[t], 0.0).astype(BF16)
+        for t in (1, 0):
+            rows = pl.ds(128 * t, 128)
+            for yt in order:
+                send(acc.at[ph, 2 * yt + 1 - k, rows], drecv.at[ph, yt, rows], (ds.at[ph, t, yt], dr.at[ph, t, yt]), partner)
+
+        def paired(t, yt):
+            rows = pl.ds(128 * t, 128)
+            got(drecv.at[ph, yt, rows], (ds.at[ph, t, yt], dr.at[ph, t, yt]), partner)
+            return acc[ph, 2 * yt + k, rows] + drecv[ph, yt, rows]
+
+        for t in (1, 0):
+            for d, yt in zip((2, 1, 3), order):
+                ysend[ph, t, d - 1] = paired(t, yt).astype(BF16)
+                part = (ysend.at[ph, t, d - 1], yrecv.at[ph, t, d - 1])
+                send(*part, (ys.at[ph, t, d - 1], yr.at[ph, t, d - 1]), ypeer[d - 1])
+        for t in (1, 0):
+            total = paired(t, y)
+            for d in (1, 3, 2):
+                got(yrecv.at[ph, t, d - 1], (ys.at[ph, t, d - 1], yr.at[ph, t, d - 1]), ypeer[d - 1])
+                total = total + yrecv[ph, t, d - 1].astype(F32)
+            finish(t, total)
+
+    def squared(t, total):
+        block = jnp.where(tab[me_r, 34] > t, total, 0.0).astype(BF16)
         sown[t] = block
+        launch(1, t, sown.at[t])
         out_ref[t] = block
-    second = phase(1, sown.at[0], sown.at[1])
-    for t in range(2):
-        mixed = 1.5 * xs[tab[me_r, 32 + t]].astype(F32) - 0.5 * second[t]
-        out_ref[2 + t] = jnp.where(count > t, mixed, 0.0).astype(BF16)
+
+    def mixed(t, total):
+        value = 1.5 * xs[tab[me_r, 32 + t]].astype(F32) - 0.5 * total
+        out_ref[2 + t] = jnp.where(tab[me_r, 34] > t, value, 0.0).astype(BF16)
+
+    launch(0, 1, x_hbm.at[1])
+    launch(0, 0, x_hbm.at[0])
+    phase(0, squared)
+    phase(1, mixed)
     for copy in pending:
         copy.wait_send()
 
@@ -304,8 +315,8 @@
             pltpu.VMEM((2, 8, 256, 128), F32),
             pltpu.VMEM((2, 128, 128), BF16),
             pltpu.VMEM((2, NY, 256, 128), F32),
-            pltpu.VMEM((2, NY - 1, 256, 128), BF16),
-            pltpu.VMEM((2, NY - 1, 256, 128), BF16),
+            pltpu.VMEM((2, 2, NY - 1, 128, 128), BF16),
+            pltpu.VMEM((2, 2, NY - 1, 128, 128), BF16),
             pltpu.VMEM((8, 128), I32),
             pltpu.SMEM((8, 128), I32),
             dma, dma, dma((4,)),
@@ -314,8 +325,8 @@
             dma((2, 2, 4, NY)), dma((2, 2, 4, NY)),
             dma((2, 8)), dma((2, 8)),
             dma((2, 3, NZ)), dma((2, 3, NZ)),
-            dma((2, NY)), dma((2, NY)),
-            dma((2, NY - 1)), dma((2, NY - 1)),
+            dma((2, 2, NY)), dma((2, 2, NY)),
+            dma((2, 2, NY - 1)), dma((2, 2, NY - 1)),
         ],
         compiler_params=pltpu.CompilerParams(collective_id=0, has_side_effects=True),
     )(x_slots, x_count, s_slots.transpose(0, 2, 1), s_count, x_blocks.reshape(CAPX, 128, 128))

time: 78.3 us -> 75.9 us (0.969)
  Pallas kernels: 77.5 us -> 75.2 us
    pallas_call x1, Pallas kernels: 76 us -> 73.6 us  [local(): pl.pallas_call(kernel, out_shape=jax.ShapeDtypeStruct((4, 128, 128), BF16...]
where the time goes in v4:
time: 75.9 us; the launch traced here: 75.8 us
  Pallas kernels  75.2 us (99%)
    pallas_call x1, Pallas kernels, local(): pl.pallas_call(kernel, out_shape=jax.ShapeDtypeStruct((4, 128, 128), BF16...  73.6 us
    pallas_call x1, Pallas kernels, local(): pl.pallas_call(split, out_shape=(part, part), in_specs=[vmem], out_specs=...  1.56 us

profile of v4, /device:TPU:1, one launch (start us, length us, event | category | flops | bytes accessed | tf_op | source)
XLA Modules:
  0.0 75.8 jit_solution(643728825095621481)
XLA Ops:
  0.6 73.6 %shard_map.68.both = bf16[4,128,128]{2,1,0:T(8,128)(2,1)} custom-call(s32[8,32,42]{2,1,0:T(8,128)} %x_slots_hbm.1, s32[8,32]{1,0:T(8,128)} %x_count_hbm.1, s32[8,2,32]{2,1,0:T(2,128)} %bitcast.5, s32[8,32]{1,0:T(8,128)} %s_count_hbm.1, bf16[42,128,128]{2,1,0:T(8,128)(2,1)} %bitcast.4), custom_call_target="tpu_custom_call" | custom-call | tf_op jit(solution)/shard_map/pallas_call | solution.py:303
  74.3 1.6 %shard_map.69 = (bf16[2,128,128]{2,1,0:T(8,128)(2,1)}, bf16[2,128,128]{2,1,0:T(8,128)(2,1)}) custom-call(bf16[4,128,128]{2,1,0:T(8,128)(2,1)} %shard_map.68.both), custom_call_target="tpu_custom_call" | custom-call | tf_op jit(solution)/shard_map/pallas_call | solution.py:334

commit v5 on v4

--- a/solution.py
+++ b/solution.py
@@ -292,17 +292,12 @@
         copy.wait_send()
 
 
-def split(both, square, result):
-    square[...] = both[:2]
-    result[...] = both[2:]
-
-
 def local(x_blocks, x_slots, x_count, s_slots, s_count):
     dma = pltpu.SemaphoreType.DMA
     vmem = pl.BlockSpec(memory_space=pltpu.VMEM)
     both = pl.pallas_call(
         kernel,
-        out_shape=jax.ShapeDtypeStruct((4, 128, 128), BF16),
+        out_shape=pltpu.VMEM((4, 128, 128), BF16),
         in_specs=[pl.BlockSpec(memory_space=pl.ANY)] * 5,
         out_specs=vmem,
         scratch_shapes=[
@@ -330,10 +325,7 @@
         ],
         compiler_params=pltpu.CompilerParams(collective_id=0, has_side_effects=True),
     )(x_slots, x_count, s_slots.transpose(0, 2, 1), s_count, x_blocks.reshape(CAPX, 128, 128))
-    part = jax.ShapeDtypeStruct((2, 128, 128), BF16)
-    square, result = pl.pallas_call(
-        split, out_shape=(part, part), in_specs=[vmem], out_specs=(vmem, vmem)
-    )(both)
+    square, result = both[:2], both[2:]
     return square[None, None], result[None, None]
 
 

time: 75.9 us -> 74.4 us (0.980)
  Pallas kernels: 75.2 us -> 73 us
    pallas_call x2 -> x1, Pallas kernels: 75.2 us -> 73 us  [local(): pl.pallas_call(kernel, out_shape=pltpu.VMEM((4, 128, 128), BF16), in_spec...]
where the time goes in v5:
time: 74.4 us; the launch traced here: 74.3 us
  Pallas kernels  73 us (98%)
    pallas_call x1, Pallas kernels, local(): pl.pallas_call(kernel, out_shape=pltpu.VMEM((4, 128, 128), BF16), in_spec...  73 us

profile of v5, /device:TPU:1, one launch (start us, length us, event | category | flops | bytes accessed | tf_op | source)
XLA Modules:
  0.0 74.3 jit_solution(17553926926297138975)
XLA Ops:
  0.6 73.0 %shard_map.68 = bf16[4,128,128]{2,1,0:T(8,128)(2,1)S(1)} custom-call(s32[8,32,42]{2,1,0:T(8,128)} %x_slots_hbm.1, s32[8,32]{1,0:T(8,128)} %x_count_hbm.1, s32[8,2,32]{2,1,0:T(2,128)} %bitcast.7, s32[8,32]{1,0:T(8,128)} %s_count_hbm.1, bf16[42,128,128]{2,1,0:T(8,128)(2,1)} %bitcast.6), custom_call_target="tpu_custom_call" | custom-call | tf_op jit(solution)/shard_map/pallas_call | solution.py:298
  73.6 0.7 slice_bitcast_fusion

commit v6 on v5

--- a/solution.py
+++ b/solution.py
@@ -108,6 +108,7 @@
     xs[CAPX] = jnp.zeros((128, 128), BF16)
     pl.semaphore_wait(barrier, len(everyone))
 
+    nearest = [(y + d) % NY for d in (0, 1, 3, 2)]
     pending = []
 
     def remote(src, dst, sems, peer):
@@ -210,7 +211,7 @@
         for i, d in ((2, 2), (3, -2), (0, 1), (1, -1)):
             send_b(z, i, i)
         cast(z, True)
-        for yi in range(NY):
+        for yi in nearest:
             got(block(z, yi, 0), (as_.at[ph, 0], ar.at[ph, yi]), partner)
             ring(0, 0, yi)
             ring(0, 1, yi)
@@ -224,12 +225,12 @@
             cast(near(d), True)
 
         def advance(step):
-            for yi in range(NY):
+            for place, yi in enumerate(nearest):
                 for way in range(2):
-                    if step == 3 and way != yi // 2:
+                    if step == 3 and way != place // 2:
                         continue
                     ring_got(step, way, yi)
-                    if step < 2 or (step == 2 and way == yi // 2):
+                    if step < 2 or (step == 2 and way == place // 2):
                         ring(step + 1, way, yi)
 
         advance(0)

time: 74.4 us -> 73.8 us (level)
  no operation moved by 1% of the time
where the time goes in v6:
time: 73.8 us; the launch traced here: 73.7 us
  Pallas kernels  72.4 us (98%)
    pallas_call x1, Pallas kernels, local(): pl.pallas_call(kernel, out_shape=pltpu.VMEM((4, 128, 128), BF16), in_spec...  72.4 us

profile of v6, /device:TPU:1, one launch (start us, length us, event | category | flops | bytes accessed | tf_op | source)
XLA Modules:
  0.0 73.7 jit_solution(15618170369278665741)
XLA Ops:
  0.6 72.4 %shard_map.68 = bf16[4,128,128]{2,1,0:T(8,128)(2,1)S(1)} custom-call(s32[8,32,42]{2,1,0:T(8,128)} %x_slots_hbm.1, s32[8,32]{1,0:T(8,128)} %x_count_hbm.1, s32[8,2,32]{2,1,0:T(2,128)} %bitcast.7, s32[8,32]{1,0:T(8,128)} %s_count_hbm.1, bf16[42,128,128]{2,1,0:T(8,128)(2,1)} %bitcast.6), custom_call_target="tpu_custom_call" | custom-call | tf_op jit(solution)/shard_map/pallas_call | solution.py:299
  73.1 0.7 slice_bitcast_fusion
